TPU v7x, 32 devices: a whole 2x2x4 slice. The times are simulated.
32 devices in a mesh: gy: 8 (over z, x), gz: 4 (over y, core).
Axes of the slice: x: 2, y: 2, z: 4, core: 2. Of those that a mesh axis runs over, the one named last changes fastest.
Arguments:
- fraction: float32 [64, 64, 1024], P('gz', 'gy'), may hold values from 0 to 1
- velocity_x: float32 [64, 64, 1024], P('gz', 'gy'), may hold values from -9 to 9
- velocity_y: float32 [64, 64, 1024], P('gz', 'gy'), may hold values from -9 to 9
- velocity_z: float32 [64, 64, 1024], P('gz', 'gy'), may hold values from -9 to 9
Outputs:
- advected: float32 [64, 64, 1024], P('gz', 'gy')
- time_step: float32 [], replicated
All inputs are finite; a program needn't handle non-finite values. Where the computation divides by a largest or mean magnitude, that divisor is 1e-20 or more.
Results may differ from a plain program's by a relative error of at most 0.0003.
Values sent between devices are 32-bit elements; how exact they have to be, the bound alone decides.
A program may use at most 64 MiB of HBM per device.

v0:
```python
import jax
import jax.numpy as jnp
from jax import lax
from jax.sharding import PartitionSpec as P

NEWTON = 5


tilt_floor = 0.1
courant = 0.45
epsilon = 1e-06


def extended(block, sides, width):
    for axis, dim in sides:
        count = lax.axis_size(axis)
        forward = [(i, i + 1) for i in range(count - 1)]
        forward.append((count - 1, 0))
        backward = [(target, source) for source, target in forward]
        low = lax.ppermute(
            lax.slice_in_dim(block, block.shape[dim] - width, None, axis=dim), axis, forward
        )
        high = lax.ppermute(lax.slice_in_dim(block, 0, width, axis=dim), axis, backward)
        block = jnp.concatenate([low, block, high], axis=dim)
    return block


def shifted(value, axis, steps):
    count = lax.axis_size(axis)
    pairs = [(source, (source + steps) % count) for source in range(count)]
    return lax.ppermute(value, axis, pairs)


def cube_step(reach, height):
    safe = jnp.where(height > 0, height, 1.0)
    whole = 3.0 * reach * reach - 3.0 * reach * height + height * height
    partial_part = reach * reach * reach / safe
    return jnp.where(reach - height >= 0, whole, jnp.where(reach >= 0, partial_part, 0.0))


def cube_rate(reach, height):
    safe = jnp.where(height > 0, height, 1.0)
    whole = 6.0 * reach - 3.0 * height
    partial_part = 3.0 * reach * reach / safe
    return jnp.where(reach - height >= 0, whole, jnp.where(reach >= 0, partial_part, 0.0))


def region_volume(offset, tilt_a, tilt_b, height, extent):
    combo = (
        cube_step(offset, height)
        - cube_step(offset - tilt_a, height)
        - cube_step(offset - tilt_b, height)
        + cube_step(offset - tilt_a - tilt_b, height)
    )
    return extent * combo / (6.0 * tilt_a * tilt_b)


def section_area(offset, tilt_a, tilt_b, height):
    combo = (
        cube_rate(offset, height)
        - cube_rate(offset - tilt_a, height)
        - cube_rate(offset - tilt_b, height)
        + cube_rate(offset - tilt_a - tilt_b, height)
    )
    return combo / (6.0 * tilt_a * tilt_b)


def youngs_slope(padded):

    def smooth_zero(arr):
        return arr[:-2] + 2.0 * arr[1:-1] + arr[2:]

    def smooth_one(arr):
        return arr[:, :-2] + 2.0 * arr[:, 1:-1] + arr[:, 2:]

    def smooth_cells(arr):
        return jnp.roll(arr, 1, 2) + 2.0 * arr + jnp.roll(arr, -1, 2)

    diff_zero = padded[2:] - padded[:-2]
    diff_one = padded[:, 2:] - padded[:, :-2]
    diff_cells = jnp.roll(padded, -1, 2) - jnp.roll(padded, 1, 2)
    grad_zero = smooth_cells(smooth_one(diff_zero)) / 32.0
    grad_one = smooth_cells(smooth_zero(diff_one)) / 32.0
    grad_cells = smooth_one(smooth_zero(diff_cells)) / 32.0
    return (grad_zero, grad_one, grad_cells)


def plane_for(fraction, slopes, axis_dim):
    slope_d = slopes[axis_dim]
    across = [slopes[index] for index in range(3) if index != axis_dim]
    tilt_d = jnp.abs(slope_d)
    tilt_a = jnp.abs(across[0]) + tilt_floor
    tilt_b = jnp.abs(across[1]) + tilt_floor
    volume = jnp.clip(fraction, 0.0, 1.0)
    lesser = jnp.minimum(volume, 1.0 - volume)
    summed = tilt_a + tilt_b + tilt_d
    offset = 0.5 * summed
    for repeat in range(NEWTON):
        offset = offset - (
            region_volume(offset, tilt_a, tilt_b, tilt_d, 1.0) - lesser
        ) / section_area(offset, tilt_a, tilt_b, tilt_d)
    offset = jnp.where(volume > 0.5, summed - offset, offset)
    return (offset, tilt_a, tilt_b, tilt_d, slope_d > 0)


def outflow(planes, width, upward):
    offset, tilt_a, tilt_b, tilt_d, mirrored = planes
    if upward:
        start_at = jnp.where(mirrored, 0.0, 1.0 - width)
    else:
        start_at = jnp.where(mirrored, 1.0 - width, 0.0)
    return region_volume(offset - tilt_d * start_at, tilt_a, tilt_b, tilt_d * width, width)


def take_rows(arr, first_row, limit_row, axis_dim):
    return lax.slice_in_dim(arr, first_row, limit_row, axis=axis_dim)


def sweep_cells(fraction, velocity, time_step):
    padded = extended(fraction, (("gy", 1), ("gz", 0)), 1)
    planes = plane_for(fraction, youngs_slope(padded), 2)
    velocity_low = jnp.roll(velocity, 1, 2)
    out_upper = outflow(planes, jnp.maximum(time_step * velocity, 0.0), True)
    out_lower = outflow(planes, jnp.maximum(-time_step * velocity_low, 0.0), False)
    from_below = jnp.roll(out_upper, 1, 2)
    from_above = jnp.roll(out_lower, -1, 2)
    divisor = 1.0 - time_step * velocity + time_step * velocity_low
    return (fraction - out_upper - out_lower + from_below + from_above) / divisor


def pass_rows(upper_row, lower_row, axis_dim):
    if axis_dim == 1:
        from_below = shifted(upper_row, "gy", 1)
        from_above = shifted(lower_row, "gy", -1)
    else:
        from_below = shifted(upper_row, "gz", 1)
        from_above = shifted(lower_row, "gz", -1)
    return (from_below, from_above)


def sweep_outflow(fraction, velocity, lower_row, axis_dim, time_step):
    padded = extended(fraction, (("gy", 1), ("gz", 0)), 1)
    planes = plane_for(fraction, youngs_slope(padded), axis_dim)
    cells_d = velocity.shape[axis_dim]
    velocity_low = jnp.concatenate(
        [lower_row, take_rows(velocity, 0, cells_d - 1, axis_dim)], axis=axis_dim
    )
    out_upper = outflow(planes, jnp.maximum(time_step * velocity, 0.0), True)
    out_lower = outflow(planes, jnp.maximum(-time_step * velocity_low, 0.0), False)
    edge_below, edge_above = pass_rows(
        take_rows(out_upper, cells_d - 1, cells_d, axis_dim),
        take_rows(out_lower, 0, 1, axis_dim),
        axis_dim,
    )
    from_below = jnp.concatenate(
        [edge_below, take_rows(out_upper, 0, cells_d - 1, axis_dim)], axis=axis_dim
    )
    from_above = jnp.concatenate(
        [take_rows(out_lower, 1, cells_d, axis_dim), edge_above], axis=axis_dim
    )
    divisor = 1.0 - time_step * velocity + time_step * velocity_low
    return (fraction - out_upper - out_lower + from_below + from_above) / divisor


def shards(fraction, velocity_x, velocity_y, velocity_z):
    cells_all = float(fraction.size * lax.axis_size("gy") * lax.axis_size("gz"))
    local_peak = jnp.maximum(
        jnp.maximum(jnp.max(jnp.abs(velocity_x)), jnp.max(jnp.abs(velocity_y))),
        jnp.max(jnp.abs(velocity_z)),
    )
    local_share = jnp.sum(4.0 * fraction * (1.0 - fraction))
    umax = lax.pmax(local_peak, ("gy", "gz"))
    share_sum = lax.psum(local_share, ("gy", "gz"))
    time_step = courant / ((umax + epsilon) * (1.0 + share_sum / cells_all))
    rows_y = velocity_y.shape[1]
    planes_z = velocity_z.shape[0]
    lower_y = shifted(take_rows(velocity_y, rows_y - 1, rows_y, 1), "gy", 1)
    lower_z = shifted(take_rows(velocity_z, planes_z - 1, planes_z, 0), "gz", 1)
    field = sweep_cells(fraction, velocity_x, time_step)
    field = sweep_outflow(field, velocity_y, lower_y, 1, time_step)
    field = sweep_outflow(field, velocity_z, lower_z, 0, time_step)
    return (field, time_step)


def solution(mesh):
    in_specs = (P("gz", "gy", None), P("gz", "gy", None), P("gz", "gy", None), P("gz", "gy", None))
    out_specs = (P("gz", "gy", None), P())
    return jax.shard_map(shards, mesh=mesh, in_specs=in_specs, out_specs=out_specs, check_vma=False)
```

profile of v0, /device:TPU:0, one launch (start us, length us, event | category | flops | bytes accessed | tf_op | source)
XLA Modules:
  0.0 179.1 jit_solution(15145708965871306312)
XLA Ops:
  0.6 1.4 fusion.863
  2.0 3.0 %collective-permute-start = (f32[16,1,1024]{2,1,0:T(1,128)S(1)}, f32[16,1,1024]{2,1,0:T(1,128)S(1)}, u32[]{:S(2)}, u32[]{:S(2)}) collective-permute-start(f32[16,1,1024]{2,1,0:T(1,128)S(1)} %get-tuple-element.57), channel_id=1, source_target_pairs={{0,4},{4,8},{8,12},{12,16},{16,20},{20,24},{24,28},{28,0},{1,5},{5... | collective-permute-start | bytes 196616 | tf_op jit(solution)/shard_map/ppermute | solution.py:20
  5.1 3.1 %collective-permute-start.1 = (f32[16,1,1024]{2,1,0:T(1,128)S(1)}, f32[16,1,1024]{2,1,0:T(1,128)S(1)}, u32[]{:S(2)}, u32[]{:S(2)}) collective-permute-start(f32[16,1,1024]{2,1,0:T(1,128)S(1)} %get-tuple-element.58), channel_id=1, source_target_pairs={{4,0},{8,4},{12,8},{16,12},{20,16},{24,20},{28,24},{0,28},{5,1},{9... | collective-permute-start | bytes 196616 | tf_op jit(solution)/shard_map/ppermute | solution.py:23
  8.2 1.7 abs_reduce_fusion.1
  9.8 1.8 abs_reduce_fusion.2
  11.6 0.6 abs_reduce_fusion
  14.2 0.7 collective-permute-start.2
  14.9 0.7 multiply_reduce_fusion
  15.6 37.7 %pmax.7 = f32[]{:T(128)} all-reduce(f32[]{:T(128)S(6)} %max.35), channel_id=1, replica_groups=mesh['gy'=8,'gz'=4] {'gy','gz'}, use_global_device_ids=true, to_apply=%region_3.0 | all-reduce | flops 1 | bytes 8 | tf_op jit(solution)/shard_map/pmax | solution.py:172
  53.4 41.7 %psum.7 = f32[]{:T(128)} all-reduce(f32[]{:T(128)} %multiply_reduce_fusion), channel_id=1, replica_groups=mesh['gy'=8,'gz'=4] {'gy','gz'}, use_global_device_ids=true, to_apply=%region_5.0 | all-reduce | flops 1 | bytes 8 | tf_op jit(solution)/shard_map/psum | solution.py:173
  96.7 0.4 fusion.848
  97.3 0.2 fusion.14
  97.7 0.4 fusion.860
  98.2 0.5 fusion.7
  98.9 11.0 %fusion.133 = (f32[16,8,1024]{2,1,0:T(8,128)S(1)}, f32[16,8,1024]{2,1,0:T(8,128)S(1)}, f32[16,8,1024]{2,1,0:T(8,128)S(1)}, f32[16,8,1024]{2,1,0:T(8,128)S(1)}, f32[16,8,1024]{2,1,0:T(8,128)S(1)}) fusion(f32[16,8,1023]{2,1,0:T(8,128)S(1)} %bitcast.4, f32[16,8,1]{2,1,0:T(8,128)S(1)} %slice.388, f32[]{:T(128)S(6)} %neg.2, f32[16,8,1024]{2,1,0:T(8,128)S(1)} %copy-done, ...), kind=kLoop, calls=%fused_computation.450 | loop fusion | flops 71303168 | bytes 10485764 | tf_op jit(solution)/shard_map/div | solution.py:55
  110.1 1.3 fusion.118
  111.5 0.5 fusion.592
  112.0 2.3 %collective-permute-start.4 = (f32[16,1,1024]{2,1,0:T(1,128)S(1)}, f32[16,1,1024]{2,1,0:T(1,128)S(1)}, u32[]{:S(2)}, u32[]{:S(2)}) collective-permute-start(f32[16,1,1024]{2,1,0:T(1,128)S(1)} %get-tuple-element.47), channel_id=1, source_target_pairs={{0,4},{4,8},{8,12},{12,16},{16,20},{20,24},{24,28},{28,0},{1,5},{5... | collective-permute-start | bytes 196616 | tf_op jit(solution)/shard_map/ppermute | solution.py:20
  114.4 2.4 %collective-permute-start.5 = (f32[16,1,1024]{2,1,0:T(1,128)S(1)}, f32[16,1,1024]{2,1,0:T(1,128)S(1)}, u32[]{:S(2)}, u32[]{:S(2)}) collective-permute-start(f32[16,1,1024]{2,1,0:T(1,128)S(1)} %get-tuple-element.48), channel_id=1, source_target_pairs={{4,0},{8,4},{12,8},{16,12},{20,16},{24,20},{28,24},{0,28},{5,1},{9... | collective-permute-start | bytes 196616 | tf_op jit(solution)/shard_map/ppermute | solution.py:23
  116.8 2.3 %collective-permute-done.4 = f32[16,1,1024]{2,1,0:T(1,128)S(1)} collective-permute-done((f32[16,1,1024]{2,1,0:T(1,128)S(1)}, f32[16,1,1024]{2,1,0:T(1,128)S(1)}, u32[]{:S(2)}, u32[]{:S(2)}) %collective-permute-start.4) | collective-permute-done | bytes 65568 | tf_op jit(solution)/shard_map/ppermute | solution.py:20
  119.4 0.5 collective-permute-start.7
  120.0 0.5 collective-permute-start.8
  120.5 0.8 collective-permute-done.6
  121.3 2.9 %collective-permute-done.7 = f32[1,10,1024]{2,1,0:T(8,128)S(1)} collective-permute-done((f32[1,10,1024]{2,1,0:T(8,128)S(1)}, f32[1,10,1024]{2,1,0:T(8,128)S(1)}, u32[]{:S(2)}, u32[]{:S(2)}) %collective-permute-start.7) | collective-permute-done | bytes 40992 | tf_op jit(solution)/shard_map/ppermute | solution.py:20
  124.4 0.4 fusion.847
  125.0 0.2 fusion.855
  125.3 0.5 fusion.4
  126.0 0.2 fusion.12
  126.3 0.2 fusion.857
  126.6 0.6 collective-permute-done.8
  127.2 10.9 %fusion.259 = (f32[16,8,1024]{2,1,0:T(8,128)S(1)}, f32[16,8,1024]{2,1,0:T(8,128)S(1)}, f32[16,8,1024]{2,1,0:T(8,128)S(1)}, f32[16,8,1024]{2,1,0:T(8,128)S(1)}, f32[16,8,1024]{2,1,0:T(8,128)S(1)}) fusion(f32[16,7,1024]{2,1,0:T(8,128)S(1)} %bitcast.6, f32[16,1,1024]{2,1,0:T(1,128)S(1)} %collective-permute-done.8, f32[]{:T(128)S(6)} %neg.2, ...), kind=kLoop, calls=%fused_computation.580 | loop fusion | flops 71303168 | bytes 10485764 | tf_op jit(solution)/shard_map/div | solution.py:55
  138.1 1.3 fusion.244
  139.6 4.8 %collective-permute-start.10 = (f32[16,1,1024]{2,1,0:T(1,128)S(1)}, f32[16,1,1024]{2,1,0:T(1,128)S(1)}, u32[]{:S(2)}, u32[]{:S(2)}) collective-permute-start(f32[16,1,1024]{2,1,0:T(1,128)S(1)} %slice.527), channel_id=1, source_target_pairs={{0,28},{4,0},{8,4},{12,8},{16,12},{20,16},{24,20},{28,24},{1,29},{... | collective-permute-start | bytes 196616 | tf_op jit(solution)/shard_map/ppermute | solution.py:31
  144.4 2.8 %collective-permute-done.9 = f32[16,1,1024]{2,1,0:T(1,128)S(1)} collective-permute-done((f32[16,1,1024]{2,1,0:T(1,128)S(1)}, f32[16,1,1024]{2,1,0:T(1,128)S(1)}, u32[]{:S(2)}, u32[]{:S(2)}) %collective-permute-start.9) | collective-permute-done | bytes 65568 | tf_op jit(solution)/shard_map/ppermute | solution.py:31
  147.1 0.5 fusion.600
  147.8 4.7 %collective-permute-start.12 = (f32[16,1,1024]{2,1,0:T(1,128)S(1)}, f32[16,1,1024]{2,1,0:T(1,128)S(1)}, u32[]{:S(2)}, u32[]{:S(2)}) collective-permute-start(f32[16,1,1024]{2,1,0:T(1,128)S(1)} %get-tuple-element.38), channel_id=1, source_target_pairs={{4,0},{8,4},{12,8},{16,12},{20,16},{24,20},{28,24},{0,28},{5,1},{9... | collective-permute-start | bytes 196616 | tf_op jit(solution)/shard_map/ppermute | solution.py:23
  152.5 2.2 %collective-permute-done.11 = f32[16,1,1024]{2,1,0:T(1,128)S(1)} collective-permute-done((f32[16,1,1024]{2,1,0:T(1,128)S(1)}, f32[16,1,1024]{2,1,0:T(1,128)S(1)}, u32[]{:S(2)}, u32[]{:S(2)}) %collective-permute-start.11) | collective-permute-done | bytes 65568 | tf_op jit(solution)/shard_map/ppermute | solution.py:20
  154.8 1.7 collective-permute-start.14
  156.6 1.9 %collective-permute-done.13 = f32[1,10,1024]{2,1,0:T(8,128)S(1)} collective-permute-done((f32[1,10,1024]{2,1,0:T(8,128)S(1)}, f32[1,10,1024]{2,1,0:T(8,128)S(1)}, u32[]{:S(2)}, u32[]{:S(2)}) %collective-permute-start.13) | collective-permute-done | bytes 40992 | tf_op jit(solution)/shard_map/ppermute | solution.py:20
  158.5 0.2 fusion.9
  159.4 0.4 fusion.846
  159.9 0.5 fusion.1
  160.7 0.2 fusion.852
  161.0 10.9 %fusion.385 = (f32[16,8,1024]{2,1,0:T(8,128)S(1)}, f32[16,8,1024]{2,1,0:T(8,128)S(1)}, f32[16,8,1024]{2,1,0:T(8,128)S(1)}, f32[16,8,1024]{2,1,0:T(8,128)S(1)}, f32[16,8,1024]{2,1,0:T(8,128)S(1)}) fusion(f32[15,8,1024]{2,1,0:T(8,128)S(1)} %slice.465, f32[1,8,1024]{2,1,0:T(8,128)S(1)} %collective-permute-done.15, f32[]{:T(128)S(6)} %neg.2, ...), kind=kLoop, calls=%fused_computation.710 | loop fusion | flops 71303168 | bytes 10485764 | tf_op jit(solution)/shard_map/div | solution.py:55
  171.9 1.3 fusion.370
  173.2 2.0 %collective-permute-start.16 = (f32[1,8,1024]{2,1,0:T(8,128)S(1)}, f32[1,8,1024]{2,1,0:T(8,128)S(1)}, u32[]{:S(2)}, u32[]{:S(2)}) collective-permute-start(f32[1,8,1024]{2,1,0:T(8,128)S(1)} %slice.554), channel_id=1, source_target_pairs={{0,1},{1,2},{2,3},{3,0},{4,5},{5,6},{6,7},{7,4},{8,9},{9,10},{10,1... | collective-permute-start | bytes 98312 | tf_op jit(solution)/shard_map/ppermute | solution.py:31
  175.3 1.3 collective-permute-done.16
  176.8 1.2 fusion.608
  (65 shorter events, 4.2 us)
Async XLA Ops:
  0.6 13.5 %copy-start = (f32[16,8,1024]{2,1,0:T(8,128)S(1)}, f32[16,8,1024]{2,1,0:T(8,128)}, u32[]{:S(2)}) copy-start(f32[16,8,1024]{2,1,0:T(8,128)} %param.4) | copy-start | bytes 1572868
  0.6 11.0 %copy-start.3 = (f32[16,8,1024]{2,1,0:T(8,128)S(1)}, f32[16,8,1024]{2,1,0:T(8,128)}, u32[]{:S(2)}) copy-start(f32[16,8,1024]{2,1,0:T(8,128)} %param.7) | copy-start | bytes 1572868
  2.0 12.1 %collective-permute-start = (f32[16,1,1024]{2,1,0:T(1,128)S(1)}, f32[16,1,1024]{2,1,0:T(1,128)S(1)}, u32[]{:S(2)}, u32[]{:S(2)}) collective-permute-start(f32[16,1,1024]{2,1,0:T(1,128)S(1)} %get-tuple-element.57), channel_id=1, source_target_pairs={{0,4},{4,8},{8,12},{12,16},{16,20},{20,24},{24,28},{28,0},{1,5},{5... | collective-permute-start | bytes 196616 | tf_op jit(solution)/shard_map/ppermute | solution.py:20
  5.1 9.1 %collective-permute-start.1 = (f32[16,1,1024]{2,1,0:T(1,128)S(1)}, f32[16,1,1024]{2,1,0:T(1,128)S(1)}, u32[]{:S(2)}, u32[]{:S(2)}) collective-permute-start(f32[16,1,1024]{2,1,0:T(1,128)S(1)} %get-tuple-element.58), channel_id=1, source_target_pairs={{4,0},{8,4},{12,8},{16,12},{20,16},{24,20},{28,24},{0,28},{5,1},{9... | collective-permute-start | bytes 196616 | tf_op jit(solution)/shard_map/ppermute | solution.py:23
  9.8 85.2 %copy-start.1 = (f32[16,8,1024]{2,1,0:T(8,128)S(1)}, f32[16,8,1024]{2,1,0:T(8,128)}, u32[]{:S(2)}) copy-start(f32[16,8,1024]{2,1,0:T(8,128)} %param.5) | copy-start | bytes 1572868
  14.2 82.3 %collective-permute-start.2 = (f32[1,10,1024]{2,1,0:T(8,128)S(1)}, f32[1,10,1024]{2,1,0:T(8,128)S(1)}, u32[]{:S(2)}, u32[]{:S(2)}) collective-permute-start(f32[1,10,1024]{2,1,0:T(8,128)S(1)} %get-tuple-element.27), channel_id=1, source_target_pairs={{1,0},{2,1},{3,2},{0,3},{5,4},{6,5},{7,6},{4,7},{9,8},{10,9},{11,1... | collective-permute-start | bytes 122888 | tf_op jit(solution)/shard_map/ppermute | solution.py:23
  14.9 81.6 %collective-permute-start.3 = (f32[1,10,1024]{2,1,0:T(8,128)S(1)}, f32[1,10,1024]{2,1,0:T(8,128)S(1)}, u32[]{:S(2)}, u32[]{:S(2)}) collective-permute-start(f32[1,10,1024]{2,1,0:T(8,128)S(1)} %get-tuple-element.28), channel_id=1, source_target_pairs={{0,1},{1,2},{2,3},{3,0},{4,5},{5,6},{6,7},{7,4},{8,9},{9,10},{10,1... | collective-permute-start | bytes 122888 | tf_op jit(solution)/shard_map/ppermute | solution.py:20
  111.5 8.4 %copy-start.2 = (f32[16,8,1024]{2,1,0:T(8,128)S(1)}, f32[16,8,1024]{2,1,0:T(8,128)}, u32[]{:S(2)}) copy-start(f32[16,8,1024]{2,1,0:T(8,128)} %param.6) | copy-start | bytes 1572868
  112.0 7.1 %collective-permute-start.4 = (f32[16,1,1024]{2,1,0:T(1,128)S(1)}, f32[16,1,1024]{2,1,0:T(1,128)S(1)}, u32[]{:S(2)}, u32[]{:S(2)}) collective-permute-start(f32[16,1,1024]{2,1,0:T(1,128)S(1)} %get-tuple-element.47), channel_id=1, source_target_pairs={{0,4},{4,8},{8,12},{12,16},{16,20},{20,24},{24,28},{28,0},{1,5},{5... | collective-permute-start | bytes 196616 | tf_op jit(solution)/shard_map/ppermute | solution.py:20
  114.4 5.0 %collective-permute-start.5 = (f32[16,1,1024]{2,1,0:T(1,128)S(1)}, f32[16,1,1024]{2,1,0:T(1,128)S(1)}, u32[]{:S(2)}, u32[]{:S(2)}) collective-permute-start(f32[16,1,1024]{2,1,0:T(1,128)S(1)} %get-tuple-element.48), channel_id=1, source_target_pairs={{4,0},{8,4},{12,8},{16,12},{20,16},{24,20},{28,24},{0,28},{5,1},{9... | collective-permute-start | bytes 196616 | tf_op jit(solution)/shard_map/ppermute | solution.py:23
  119.4 2.0 %collective-permute-start.6 = (f32[1,10,1024]{2,1,0:T(8,128)S(1)}, f32[1,10,1024]{2,1,0:T(8,128)S(1)}, u32[]{:S(2)}, u32[]{:S(2)}) collective-permute-start(f32[1,10,1024]{2,1,0:T(8,128)S(1)} %get-tuple-element.25), channel_id=1, source_target_pairs={{1,0},{2,1},{3,2},{0,3},{5,4},{6,5},{7,6},{4,7},{9,8},{10,9},{11,1... | collective-permute-start | bytes 122888 | tf_op jit(solution)/shard_map/ppermute | solution.py:23
  119.4 4.8 %collective-permute-start.7 = (f32[1,10,1024]{2,1,0:T(8,128)S(1)}, f32[1,10,1024]{2,1,0:T(8,128)S(1)}, u32[]{:S(2)}, u32[]{:S(2)}) collective-permute-start(f32[1,10,1024]{2,1,0:T(8,128)S(1)} %get-tuple-element.26), channel_id=1, source_target_pairs={{0,1},{1,2},{2,3},{3,0},{4,5},{5,6},{6,7},{7,4},{8,9},{9,10},{10,1... | collective-permute-start | bytes 122888 | tf_op jit(solution)/shard_map/ppermute | solution.py:20
  120.0 7.2 %collective-permute-start.8 = (f32[16,1,1024]{2,1,0:T(1,128)S(1)}, f32[16,1,1024]{2,1,0:T(1,128)S(1)}, u32[]{:S(2)}, u32[]{:S(2)}) collective-permute-start(f32[16,1,1024]{2,1,0:T(1,128)S(1)} %slice.426), channel_id=1, source_target_pairs={{0,4},{4,8},{8,12},{12,16},{16,20},{20,24},{24,28},{28,0},{1,5},{5... | collective-permute-start | bytes 196616 | tf_op jit(solution)/shard_map/ppermute | solution.py:31
  139.5 7.7 %collective-permute-start.9 = (f32[16,1,1024]{2,1,0:T(1,128)S(1)}, f32[16,1,1024]{2,1,0:T(1,128)S(1)}, u32[]{:S(2)}, u32[]{:S(2)}) collective-permute-start(f32[16,1,1024]{2,1,0:T(1,128)S(1)} %slice.524), channel_id=1, source_target_pairs={{0,4},{4,8},{8,12},{12,16},{16,20},{20,24},{24,28},{28,0},{1,5},{5... | collective-permute-start | bytes 196616 | tf_op jit(solution)/shard_map/ppermute | solution.py:31
  139.6 7.6 %collective-permute-start.10 = (f32[16,1,1024]{2,1,0:T(1,128)S(1)}, f32[16,1,1024]{2,1,0:T(1,128)S(1)}, u32[]{:S(2)}, u32[]{:S(2)}) collective-permute-start(f32[16,1,1024]{2,1,0:T(1,128)S(1)} %slice.527), channel_id=1, source_target_pairs={{0,28},{4,0},{8,4},{12,8},{16,12},{20,16},{24,20},{28,24},{1,29},{... | collective-permute-start | bytes 196616 | tf_op jit(solution)/shard_map/ppermute | solution.py:31
  147.7 7.0 %collective-permute-start.11 = (f32[16,1,1024]{2,1,0:T(1,128)S(1)}, f32[16,1,1024]{2,1,0:T(1,128)S(1)}, u32[]{:S(2)}, u32[]{:S(2)}) collective-permute-start(f32[16,1,1024]{2,1,0:T(1,128)S(1)} %get-tuple-element.37), channel_id=1, source_target_pairs={{0,4},{4,8},{8,12},{12,16},{16,20},{20,24},{24,28},{28,0},{1,5},{5... | collective-permute-start | bytes 196616 | tf_op jit(solution)/shard_map/ppermute | solution.py:20
  147.8 7.0 %collective-permute-start.12 = (f32[16,1,1024]{2,1,0:T(1,128)S(1)}, f32[16,1,1024]{2,1,0:T(1,128)S(1)}, u32[]{:S(2)}, u32[]{:S(2)}) collective-permute-start(f32[16,1,1024]{2,1,0:T(1,128)S(1)} %get-tuple-element.38), channel_id=1, source_target_pairs={{4,0},{8,4},{12,8},{16,12},{20,16},{24,20},{28,24},{0,28},{5,1},{9... | collective-permute-start | bytes 196616 | tf_op jit(solution)/shard_map/ppermute | solution.py:23
  154.8 3.7 %collective-permute-start.13 = (f32[1,10,1024]{2,1,0:T(8,128)S(1)}, f32[1,10,1024]{2,1,0:T(8,128)S(1)}, u32[]{:S(2)}, u32[]{:S(2)}) collective-permute-start(f32[1,10,1024]{2,1,0:T(8,128)S(1)} %get-tuple-element.23), channel_id=1, source_target_pairs={{0,1},{1,2},{2,3},{3,0},{4,5},{5,6},{6,7},{7,4},{8,9},{9,10},{10,1... | collective-permute-start | bytes 122888 | tf_op jit(solution)/shard_map/ppermute | solution.py:20
  154.8 3.7 %collective-permute-start.14 = (f32[1,10,1024]{2,1,0:T(8,128)S(1)}, f32[1,10,1024]{2,1,0:T(8,128)S(1)}, u32[]{:S(2)}, u32[]{:S(2)}) collective-permute-start(f32[1,10,1024]{2,1,0:T(8,128)S(1)} %get-tuple-element.24), channel_id=1, source_target_pairs={{1,0},{2,1},{3,2},{0,3},{5,4},{6,5},{7,6},{4,7},{9,8},{10,9},{11,1... | collective-permute-start | bytes 122888 | tf_op jit(solution)/shard_map/ppermute | solution.py:23
  156.6 4.4 %collective-permute-start.15 = (f32[1,8,1024]{2,1,0:T(8,128)S(1)}, f32[1,8,1024]{2,1,0:T(8,128)S(1)}, u32[]{:S(2)}, u32[]{:S(2)}) collective-permute-start(f32[1,8,1024]{2,1,0:T(8,128)S(1)} %slice.464), channel_id=1, source_target_pairs={{0,1},{1,2},{2,3},{3,0},{4,5},{5,6},{6,7},{7,4},{8,9},{9,10},{10,1... | collective-permute-start | bytes 98312 | tf_op jit(solution)/shard_map/ppermute | solution.py:31
  173.2 3.4 %collective-permute-start.16 = (f32[1,8,1024]{2,1,0:T(8,128)S(1)}, f32[1,8,1024]{2,1,0:T(8,128)S(1)}, u32[]{:S(2)}, u32[]{:S(2)}) collective-permute-start(f32[1,8,1024]{2,1,0:T(8,128)S(1)} %slice.554), channel_id=1, source_target_pairs={{0,1},{1,2},{2,3},{3,0},{4,5},{5,6},{6,7},{7,4},{8,9},{9,10},{10,1... | collective-permute-start | bytes 98312 | tf_op jit(solution)/shard_map/ppermute | solution.py:31
  175.2 1.6 collective-permute-start.17
where the time goes:
time: 181 us; the launch traced here: 179 us
  blocking collectives  79.4 us (44%)
  other arithmetic  47.8 us (26%)
  starting transfers between devices  26 us (14%)
  waiting for transfers between devices  15.2 us (8%)
  between operations  5.44 us (3%)
  local copies, waits for them, and re-layouts  5.16 us (3%)
    psum x1, blocking collectives, shards(): share_sum = lax.psum(local_share, ('gy', 'gz'))  41.7 us
    pmax x1, blocking collectives, shards(): umax = lax.pmax(local_peak, ('gy', 'gz'))  37.7 us
    div x6, other arithmetic, region_volume(): return extent * combo / (6.0 * tilt_a * tilt_b)  36.7 us
    ppermute x6, starting transfers between devices, extended(): lax.ppermute(lax.slice_in_dim(block, 0, width, axis=dim), axis, backward)  12.8 us
    ppermute x6, waiting for transfers between devices, extended(): lax.ppermute(lax.slice_in_dim(block, block.shape[dim] - width, None, axis...  9.34 us
    ppermute x6, starting transfers between devices, shifted(): return lax.ppermute(value, axis, pairs)  7.29 us
    ppermute x6, starting transfers between devices, extended(): lax.ppermute(lax.slice_in_dim(block, block.shape[dim] - width, None, axis...  5.96 us
    ppermute x6, waiting for transfers between devices, shifted(): return lax.ppermute(value, axis, pairs)  4.83 us
  transfers between devices with their start and end apart: 18, of which 10 were waited for; matrix products, arithmetic and copies ran while one was open for 6% of the time, Pallas kernels for 0%

commit v1 on v0

v1 whole, which is shorter than its diff:
```python
import functools

import jax
import jax.numpy as jnp
from jax import lax
from jax.experimental import pallas as pl
from jax.experimental.pallas import tpu as pltpu
from jax.sharding import PartitionSpec as P

NEWTON = 5
LANES = 128

tilt_floor = 0.1
courant = 0.45
epsilon = 1e-06
tiny = 1e-30

MESH = pl.DeviceIdType.MESH
SIDES = [(a, b) for a in (-1, 0, 1) for b in (-1, 0, 1) if (a, b) != (0, 0)]


def lane_of(value):
    return lax.broadcasted_iota(jnp.int32, value.shape, value.ndim - 1)


def x_next(value):
    turned = pltpu.roll(value, LANES - 1, value.ndim - 1)
    carried = pltpu.roll(turned, value.shape[-2] - 1, value.ndim - 2)
    return jnp.where(lane_of(value) == LANES - 1, carried, turned)


def x_prev(value):
    turned = pltpu.roll(value, 1, value.ndim - 1)
    carried = pltpu.roll(turned, 1, value.ndim - 2)
    return jnp.where(lane_of(value) == 0, carried, turned)


def solve_offset(g, tilt_a, tilt_b, tilt_d):
    volume = jnp.clip(g, 0.0, 1.0)
    lesser = jnp.minimum(volume, 1.0 - volume)
    low = jnp.minimum(tilt_a, tilt_b)
    high = jnp.maximum(tilt_a, tilt_b)
    n1 = jnp.minimum(low, tilt_d)
    middle = jnp.maximum(low, tilt_d)
    n2 = jnp.minimum(middle, high)
    n3 = jnp.maximum(middle, high)
    summed = tilt_a + tilt_b + tilt_d
    inverse = 1.0 / jnp.maximum(n1, tiny)
    third = inverse * (1.0 / 3.0)
    product = n2 * n3
    target = 2.0 * product * lesser
    gap = jnp.maximum(n1 + n2 - n3, 0.0)
    rate = 2.0 * n2 - 0.5 * gap * (gap * inverse)
    offset = 0.5 * summed - (product - target) / rate
    for repeat in range(NEWTON - 1):
        p1 = jnp.minimum(offset, n1)
        q1 = offset - p1
        m2 = jnp.maximum(offset - n2, 0.0)
        p2 = jnp.minimum(m2, n1)
        q2 = m2 - p2
        p3 = jnp.minimum(jnp.maximum(offset - n3, 0.0), n1)
        s1, s2, s3 = p1 * p1, p2 * p2, p3 * p3
        squares = s1 - s2 - s3
        cubes = s1 * p1 - s2 * p2 - s3 * p3
        q = q1 - q2
        rate = squares * inverse + (q + q)
        volume_part = cubes * third + q * (q1 + q2 + n1)
        offset = offset - (volume_part - target) / rate
    return jnp.where(volume > 0.5, summed - offset, offset)


def face_flux(cross, offset, tilt_a, tilt_b, slope):
    turn = slope * cross
    height = jnp.abs(turn)
    reach = offset - jnp.where(turn > 0, 0.0, jnp.abs(slope) - height)

    def parts(value):
        inside = jnp.maximum(value, 0.0)
        p = jnp.minimum(inside, height)
        q = inside - p
        return p * p * p, q * (q + height)

    reach_a = reach - tilt_a
    p0, q0 = parts(reach)
    p1, q1 = parts(reach_a)
    p2, q2 = parts(reach - tilt_b)
    p3, q3 = parts(reach_a - tilt_b)
    cubes = (p0 - p1) - (p2 - p3)
    wholes = (q0 - q1) - (q2 - q3)
    combo = cubes * ((1.0 / 3.0) / jnp.maximum(height, tiny)) + wholes
    return cross * combo / (2.0 * tilt_a * tilt_b)


def kernel(
    n_gy, n_gz, f_ref, vx_ref, vy_ref, vz_ref, out_ref, dt_ref,
    g0, g1, g2, sx, dx, off, ta, tb, sd, vx, vy, vz, fy, fz,
    fy_in, fz_in, part_y, part_z,
    halo_send, halo_recv, vel_send, vel_recv, flux_send, flux_recv,
    py_send, py_recv, pz_send, pz_recv,
):
    Z = f_ref.shape[0]
    T = sx.shape[2]
    Y = f_ref.shape[1] // T
    my = lax.axis_index("gy")
    mz = lax.axis_index("gz")

    def at(dz, dy):
        return {
            "gy": lax.rem(my + dy + n_gy, n_gy),
            "gz": lax.rem(mz + dz + n_gz, n_gz),
        }

    barrier = pltpu.get_barrier_semaphore()
    greeted = [(0, i) for i in range(1, n_gy)] + [(i, 0) for i in range(1, n_gz)]
    greeted += [(a, b) for a in (-1, 1) for b in (-1, 1)]
    for dz, dy in greeted:
        pl.semaphore_signal(barrier, inc=1, device_id=at(dz, dy), device_id_type=MESH)

    def rows_of(ref, z, y):
        return ref[z, pl.ds(y, T, stride=Y), :]

    def loop(low, high, body):
        def step(i, carry):
            body(i)
            return carry
        lax.fori_loop(low, high, step, 0)

    def span(side, count):
        if side == 0:
            return pl.ds(1, count), pl.ds(1, count)
        if side > 0:
            return pl.ds(count, 1), pl.ds(0, 1)
        return pl.ds(1, 1), pl.ds(count + 1, 1)

    def halo_copies(g, which):
        copies = []
        for index, (dz, dy) in enumerate(SIDES):
            src_z, dst_z = span(dz, Z)
            src_y, dst_y = span(dy, Y)
            copies.append(pltpu.make_async_remote_copy(
                src_ref=g.at[src_z, src_y],
                dst_ref=g.at[dst_z, dst_y],
                send_sem=halo_send.at[which, index],
                recv_sem=halo_recv.at[which, index],
                device_id=at(dz, dy),
                device_id_type=MESH,
            ))
        return copies

    def fill(z, total):
        for y in range(Y):
            f = rows_of(f_ref, z, y)
            g0[z + 1, y + 1] = f
            total = total + 4.0 * f * (1.0 - f)
        return total

    total = lax.fori_loop(0, Z, fill, jnp.zeros((T, LANES), jnp.float32))
    pl.semaphore_wait(barrier, len(greeted))
    halos0 = halo_copies(g0, 0)
    for copy in halos0:
        copy.start()

    def fill_velocity(z, peak):
        for y in range(Y):
            a = rows_of(vx_ref, z, y)
            b = rows_of(vy_ref, z, y)
            c = rows_of(vz_ref, z, y)
            vx[z, y] = a
            vy[z, y + 1] = b
            vz[z + 1, y] = c
            peak = jnp.maximum(peak, jnp.maximum(jnp.abs(a), jnp.maximum(jnp.abs(b), jnp.abs(c))))
        return peak

    peak = lax.fori_loop(0, Z, fill_velocity, jnp.zeros((T, LANES), jnp.float32))
    part_y[my, 0] = total
    part_y[my, 1] = peak
    vel_copies = [
        pltpu.make_async_remote_copy(
            src_ref=vy.at[:, pl.ds(Y, 1)], dst_ref=vy.at[:, pl.ds(0, 1)],
            send_sem=vel_send.at[0], recv_sem=vel_recv.at[0],
            device_id=at(0, 1), device_id_type=MESH,
        ),
        pltpu.make_async_remote_copy(
            src_ref=vz.at[pl.ds(Z, 1)], dst_ref=vz.at[pl.ds(0, 1)],
            send_sem=vel_send.at[1], recv_sem=vel_recv.at[1],
            device_id=at(1, 0), device_id_type=MESH,
        ),
    ]

    def part_copies(part, mine, send, recv, count, along_y):
        copies = []
        for i in range(1, count):
            copies.append(pltpu.make_async_remote_copy(
                src_ref=part.at[mine], dst_ref=part.at[mine],
                send_sem=send.at[i - 1], recv_sem=recv.at[i - 1],
                device_id=at(0, i) if along_y else at(i, 0), device_id_type=MESH,
            ))
        return copies

    y_parts = part_copies(part_y, my, py_send, py_recv, n_gy, True)
    for copy in y_parts:
        copy.start()
    for copy in vel_copies:
        copy.start()

    def smooth_rows(g, z, y, kz, ky):
        value = g[pl.ds(z, kz), pl.ds(y, ky)]
        after, before = x_next(value), x_prev(value)
        sx[pl.ds(z, kz), pl.ds(y, ky)] = before + (value + value) + after
        dx[pl.ds(z, kz), pl.ds(y, ky)] = after - before

    def smooth_inside(g):
        loop(1, Z + 1, lambda z: smooth_rows(g, z, 1, 1, Y))

    def smooth_ghosts(g):
        smooth_rows(g, 0, 0, 1, Y + 2)
        smooth_rows(g, Z + 1, 0, 1, Y + 2)

        def edge(z):
            smooth_rows(g, z, 0, 1, 1)
            smooth_rows(g, z, Y + 1, 1, 1)
        loop(1, Z + 1, edge)

    def smooth_zero(arr):
        mid = arr[1:-1]
        return (arr[:-2] + mid) + (mid + arr[2:])

    def smooth_one(arr):
        mid = arr[:, 1:-1]
        return (arr[:, :-2] + mid) + (mid + arr[:, 2:])

    def plane(g, dim, z, y, kz, ky):
        s = sx[pl.ds(z, kz + 2), pl.ds(y, ky + 2)]
        d = dx[pl.ds(z, kz + 2), pl.ds(y, ky + 2)]
        grad_zero = smooth_one(s[2:] - s[:-2]) * (1.0 / 32.0)
        across = smooth_zero(s)
        grad_one = (across[:, 2:] - across[:, :-2]) * (1.0 / 32.0)
        grad_cells = smooth_one(smooth_zero(d)) * (1.0 / 32.0)
        slopes = (grad_zero, grad_one, grad_cells)
        slope = slopes[dim]
        tilt_a, tilt_b = [jnp.abs(slopes[e]) + tilt_floor for e in range(3) if e != dim]
        value = g[pl.ds(z + 1, kz), pl.ds(y + 1, ky)]
        where = (pl.ds(z, kz), pl.ds(y, ky))
        off[where] = solve_offset(value, tilt_a, tilt_b, jnp.abs(slope))
        ta[where] = tilt_a
        tb[where] = tilt_b
        sd[where] = slope

    half = (Y - 2) // 2
    quarter = Y // 2

    def planes_inside(g, dim, low, high):
        def body(z):
            plane(g, dim, z, 1, 1, half)
            plane(g, dim, z, 1 + half, 1, Y - 2 - half)
        loop(low, high, body)

    def planes_edge(g, dim):
        for_rows_edge(lambda z, y, kz, ky: plane(g, dim, z, y, kz, ky))

    def for_rows_edge(body):
        def ends(i):
            z = i * (Z - 1)
            body(z, 0, 1, quarter)
            body(z, quarter, 1, Y - quarter)
        loop(0, 2, ends)

        def sides(i):
            z = 1 + 2 * i
            body(z, 0, 2, 1)
            body(z, Y - 1, 2, 1)
        loop(0, (Z - 2) // 2, sides)

    def for_rows_inside(body):
        def step(z):
            body(z, 1, 1, half)
            body(z, 1 + half, 1, Y - 2 - half)
        loop(1, Z - 1, step)

    def for_rows(body):
        def step(z):
            body(z, 0, 1, quarter)
            body(z, quarter, 1, Y - quarter)
        loop(0, Z, step)

    smooth_inside(g0)
    planes_inside(g0, 2, 1, Z // 2)
    for copy in y_parts:
        copy.wait()
    sums = part_y[0, 0]
    peaks = part_y[0, 1]
    for i in range(1, n_gy):
        sums = sums + part_y[i, 0]
        peaks = jnp.maximum(peaks, part_y[i, 1])
    part_z[mz, 0] = sums
    part_z[mz, 1] = peaks
    z_parts = part_copies(part_z, mz, pz_send, pz_recv, n_gz, False)
    for copy in z_parts:
        copy.start()
    planes_inside(g0, 2, Z // 2, Z - 1)
    for copy in halos0:
        copy.wait()
    smooth_ghosts(g0)
    planes_edge(g0, 2)
    for copy in z_parts:
        copy.wait()
    sums = part_z[0, 0]
    peaks = part_z[0, 1]
    for i in range(1, n_gz):
        sums = sums + part_z[i, 0]
        peaks = jnp.maximum(peaks, part_z[i, 1])
    cells_all = float(Z * Y * T * LANES * n_gy * n_gz)
    share = jnp.broadcast_to(jnp.sum(sums, keepdims=True), (T, LANES)) / cells_all
    umax = jnp.broadcast_to(jnp.max(peaks, keepdims=True), (T, LANES))
    step_value = courant / ((umax + epsilon) * (1.0 + share))
    dt_ref[0, 0] = jnp.max(step_value)
    dt = step_value[None, None]

    def x_update(z, y, kz, ky):
        where = (pl.ds(z, kz), pl.ds(y, ky))
        cross = dt * vx[where]
        upward = cross > 0

        def donor(ref):
            value = ref[where]
            return jnp.where(upward, value, x_next(value))

        flux = face_flux(cross, donor(off), donor(ta), donor(tb), donor(sd))
        value = g0[pl.ds(z + 1, kz), pl.ds(y + 1, ky)]
        g1[pl.ds(z + 1, kz), pl.ds(y + 1, ky)] = (value - flux + x_prev(flux)) / (
            1.0 - cross + x_prev(cross)
        )

    for_rows_edge(x_update)
    halos1 = halo_copies(g1, 1)
    for copy in halos1:
        copy.start()
    for_rows_inside(x_update)
    for copy in vel_copies:
        copy.wait()

    smooth_inside(g1)
    planes_inside(g1, 1, 1, Z - 1)
    for copy in halos1:
        copy.wait()
    smooth_ghosts(g1)
    planes_edge(g1, 1)

    def own_flux(velocity, where, at_face, least):
        cross = dt * velocity[at_face]
        cross = jnp.minimum(cross, 0.0) if least else jnp.maximum(cross, 0.0)
        return face_flux(cross, off[where], ta[where], tb[where], sd[where])

    def y_ends(i):
        rows = pl.ds(2 * i, 2)
        first, last = pl.ds(0, 1), pl.ds(Y - 1, 1)
        fy[rows, first] = own_flux(vy, (rows, first), (rows, first), True)
        fy[rows, pl.ds(Y, 1)] = own_flux(vy, (rows, last), (rows, pl.ds(Y, 1)), False)
    loop(0, Z // 2, y_ends)

    def flux_copies(flux, arrived, which, spans, steps):
        copies = []
        for i in range(2):
            copies.append(pltpu.make_async_remote_copy(
                src_ref=flux.at[spans[i]],
                dst_ref=arrived.at[i],
                send_sem=flux_send.at[which, i], recv_sem=flux_recv.at[which, i],
                device_id=at(*steps[i]), device_id_type=MESH,
            ))
        return copies

    every = pl.ds(0, Z)
    y_flux = flux_copies(
        fy, fy_in, 0, [(every, pl.ds(Y, 1)), (every, pl.ds(0, 1))], [(0, 1), (0, -1)]
    )
    for copy in y_flux:
        copy.start()

    def between(velocity, at_face, below, above):
        cross = dt * velocity[at_face]
        upward = cross > 0

        def donor(ref):
            return jnp.where(upward, ref[below], ref[above])

        return face_flux(cross, donor(off), donor(ta), donor(tb), donor(sd))

    def y_inside(z):
        rows = pl.ds(z, 1)
        for low, count in ((1, half), (1 + half, Y - 1 - half)):
            fy[rows, pl.ds(low, count)] = between(
                vy, (rows, pl.ds(low, count)), (rows, pl.ds(low - 1, count)), (rows, pl.ds(low, count))
            )
    loop(0, Z, y_inside)
    for copy in y_flux:
        copy.wait()

    def y_merge(i):
        rows = pl.ds(4 * i, 4)
        fy[rows, pl.ds(0, 1)] = fy[rows, pl.ds(0, 1)] + fy_in[0, rows]
        fy[rows, pl.ds(Y, 1)] = fy[rows, pl.ds(Y, 1)] + fy_in[1, rows]
    loop(0, Z // 4, y_merge)

    def y_update(z, y, kz, ky):
        rows = pl.ds(z, kz)
        low, high = pl.ds(y, ky), pl.ds(y + 1, ky)
        inside = (pl.ds(z + 1, kz), pl.ds(y + 1, ky))
        g2[inside] = (g1[inside] - fy[rows, high] + fy[rows, low]) / (
            1.0 - dt * vy[rows, high] + dt * vy[rows, low]
        )

    for_rows_edge(y_update)
    halos2 = halo_copies(g2, 2)
    for copy in halos2:
        copy.start()
    for_rows_inside(y_update)

    smooth_inside(g2)
    planes_inside(g2, 0, 1, Z - 1)
    for copy in halos2:
        copy.wait()
    smooth_ghosts(g2)
    planes_edge(g2, 0)

    def z_ends(i):
        cols = pl.ds(2 * i, 2)
        first, last = pl.ds(0, 1), pl.ds(Z - 1, 1)
        fz[first, cols] = own_flux(vz, (first, cols), (first, cols), True)
        fz[pl.ds(Z, 1), cols] = own_flux(vz, (last, cols), (pl.ds(Z, 1), cols), False)
    loop(0, Y // 2, z_ends)
    z_flux = flux_copies(fz, fz_in, 1, [(pl.ds(Z, 1),), (pl.ds(0, 1),)], [(1, 0), (-1, 0)])
    for copy in z_flux:
        copy.start()

    def z_inside(z):
        face, below = pl.ds(z, 1), pl.ds(z - 1, 1)
        for low, count in ((0, quarter), (quarter, Y - quarter)):
            cols = pl.ds(low, count)
            fz[face, cols] = between(vz, (face, cols), (below, cols), (face, cols))
    loop(1, Z, z_inside)
    for copy in z_flux:
        copy.wait()
    fz[pl.ds(0, 1)] = fz[pl.ds(0, 1)] + fz_in[0]
    fz[pl.ds(Z, 1)] = fz[pl.ds(Z, 1)] + fz_in[1]

    def z_update(z):
        for y in range(Y):
            value = (g2[z + 1, y + 1] - fz[z + 1, y] + fz[z, y]) / (
                1.0 - step_value * vz[z + 1, y] + step_value * vz[z, y]
            )
            out_ref[z, pl.ds(y, T, stride=Y), :] = value
    loop(0, Z, z_update)


def solution(mesh):
    n_gy, n_gz = mesh.shape["gy"], mesh.shape["gz"]

    def shards(*blocks):
        Z, Y, X = blocks[0].shape
        T = X // LANES

        def split(block):
            return block.reshape(Z, Y, T, LANES).transpose(0, 2, 1, 3).reshape(Z, T * Y, LANES)

        def rows(*lead):
            return pltpu.VMEM((*lead, T, LANES), jnp.float32)

        dma = pltpu.SemaphoreType.DMA
        padded = rows(Z + 2, Y + 2)
        plain = rows(Z, Y)
        field, dt = pl.pallas_call(
            functools.partial(kernel, n_gy, n_gz),
            out_shape=(
                jax.ShapeDtypeStruct((Z, T * Y, LANES), jnp.float32),
                jax.ShapeDtypeStruct((1, 1), jnp.float32),
            ),
            in_specs=[pl.BlockSpec(memory_space=pltpu.VMEM)] * 4,
            out_specs=(
                pl.BlockSpec(memory_space=pltpu.VMEM),
                pl.BlockSpec(memory_space=pltpu.SMEM),
            ),
            scratch_shapes=[
                padded, padded, padded, padded, padded,
                plain, plain, plain, plain,
                plain, rows(Z, Y + 1), rows(Z + 1, Y), rows(Z, Y + 1), rows(Z + 1, Y),
                rows(2, Z, 1), rows(2, 1, Y), rows(n_gy, 2), rows(n_gz, 2),
                dma((3, 8)), dma((3, 8)), dma((2,)), dma((2,)), dma((2, 2)), dma((2, 2)),
                dma((n_gy - 1,)), dma((n_gy - 1,)), dma((n_gz - 1,)), dma((n_gz - 1,)),
            ],
            compiler_params=pltpu.CompilerParams(
                collective_id=0, has_side_effects=True, vmem_limit_bytes=32 * 1024 * 1024
            ),
        )(*[split(block) for block in blocks])
        field = field.reshape(Z, T, Y, LANES).transpose(0, 2, 1, 3).reshape(Z, Y, X)
        return field, dt.reshape(())

    spec = P("gz", "gy", None)
    return jax.shard_map(
        shards, mesh=mesh, in_specs=(spec,) * 4, out_specs=(spec, P()), check_vma=False
    )
```

time: 181 us -> 52.9 us (0.29)
  blocking collectives: 79.4 us -> 0 us
  other arithmetic: 47.8 us -> 0 us
  Pallas kernels: 0 us -> 45.2 us
  starting transfers between devices: 26 us -> 0 us
  waiting for transfers between devices: 15.2 us -> 0 us
  between operations: 5.44 us -> 2.4 us
    pallas_call x0 -> x1, Pallas kernels: none -> 45.2 us  [shards(): pl.pallas_call(functools.partial(kernel, n_gy, n_gz), out_shape=(jax.Shap...]
    psum x1 -> x0, blocking collectives: 41.7 us -> none  [shards(): share_sum = lax.psum(local_share, ('gy', 'gz'))]
    div x9 -> x0, other arithmetic: 38.8 us -> none  [the longest x6 36.7 us: region_volume(): return extent * combo / (6.0 * tilt_a * tilt_b)]
    pmax x1 -> x0, blocking collectives: 37.7 us -> none  [shards(): umax = lax.pmax(local_peak, ('gy', 'gz'))]
    ppermute x18 -> x0, starting transfers between devices: 26 us -> none  [the longest x6 12.8 us: extended(): lax.ppermute(lax.slice_in_dim(block, 0, width, axis=dim), axis, backward)]
    ppermute x18 -> x0, waiting for transfers between devices: 15.2 us -> none  [the longest x6 9.34 us: extended(): lax.ppermute(lax.slice_in_dim(block, block.shape[dim] - width, None, axis...]
    slice x30 -> x0, local copies, waits for them, and re-layouts: 5.14 us -> none  [the longest x10 1.62 us: smooth_cells(): return jnp.roll(arr, 1, 2) + 2.0 * arr + jnp.roll(arr, -1, 2)]
    unnamed x8 -> x9, local copies, waits for them, and re-layouts: 0.02 us -> 4.95 us
  transfers between devices with their start and end apart: 18 -> 0, of which waited for: 10 -> 0; matrix products, arithmetic and copies ran while one was open for 6% -> 0% of each run, Pallas kernels for 0% -> 0%
where the time goes in v1:
time: 52.9 us; the launch traced here: 52.6 us
  Pallas kernels  45.2 us (85%)
  local copies, waits for them, and re-layouts  4.95 us (9%)
  between operations  2.4 us (5%)
    pallas_call x1, Pallas kernels, shards(): pl.pallas_call(functools.partial(kernel, n_gy, n_gz), out_shape=(jax.Shap...  45.2 us
    unnamed x9, local copies, waits for them, and re-layouts  4.95 us

profile of v1, /device:TPU:0, one launch (start us, length us, event | category | flops | bytes accessed | tf_op | source)
XLA Modules:
  0.0 52.6 jit_solution(9803595048006049528)
XLA Ops:
  0.6 0.0 copy-start
  0.6 1.0 %copy-done = f32[16,8,1024]{2,1,0:T(8,128)S(1)} copy-done((f32[16,8,1024]{2,1,0:T(8,128)S(1)}, f32[16,8,1024]{2,1,0:T(8,128)}, u32[]{:S(2)}) %copy-start) | copy-done | bytes 524312
  1.7 0.0 copy-start.1
  1.7 1.0 %copy-done.1 = f32[16,8,1024]{2,1,0:T(8,128)S(1)} copy-done((f32[16,8,1024]{2,1,0:T(8,128)S(1)}, f32[16,8,1024]{2,1,0:T(8,128)}, u32[]{:S(2)}) %copy-start.1) | copy-done | bytes 524312
  2.7 0.0 copy-start.2
  2.7 1.0 %copy-done.2 = f32[16,8,1024]{2,1,0:T(8,128)S(1)} copy-done((f32[16,8,1024]{2,1,0:T(8,128)S(1)}, f32[16,8,1024]{2,1,0:T(8,128)}, u32[]{:S(2)}) %copy-start.2) | copy-done | bytes 524312
  3.8 0.0 copy-start.3
  3.8 1.0 %copy-done.3 = f32[16,8,1024]{2,1,0:T(8,128)S(1)} copy-done((f32[16,8,1024]{2,1,0:T(8,128)S(1)}, f32[16,8,1024]{2,1,0:T(8,128)}, u32[]{:S(2)}) %copy-start.3) | copy-done | bytes 524312
  4.8 45.2 %shard_map.59 = (f32[16,64,128]{2,1,0:T(8,128)S(1)}, f32[1,1]{1,0:T(1,128)}) custom-call(f32[16,64,128]{2,1,0:T(8,128)S(1)} %bitcast.27, f32[16,64,128]{2,1,0:T(8,128)S(1)} %bitcast.28, f32[16,64,128]{2,1,0:T(8,128)S(1)} %bitcast.29, f32[16,64,128]{2,1,0:T(8,128)S(1)} %bitcast.30), custom_call_target="tpu_custom_call" | custom-call | tf_op jit(solution)/shard_map/pallas_call | solution.py:471
  50.1 0.8 %copy.8 = f32[16,8,1024]{2,1,0:T(8,128)} copy(f32[16,8,1024]{2,1,0:T(8,128)S(1)} %bitcast.26) | data formatting | bytes 1048576
Async XLA Ops:
  0.6 1.0 %copy-start = (f32[16,8,1024]{2,1,0:T(8,128)S(1)}, f32[16,8,1024]{2,1,0:T(8,128)}, u32[]{:S(2)}) copy-start(f32[16,8,1024]{2,1,0:T(8,128)} %param.4) | copy-start | bytes 1572868
  1.7 1.0 %copy-start.1 = (f32[16,8,1024]{2,1,0:T(8,128)S(1)}, f32[16,8,1024]{2,1,0:T(8,128)}, u32[]{:S(2)}) copy-start(f32[16,8,1024]{2,1,0:T(8,128)} %param.5) | copy-start | bytes 1572868
  2.7 1.0 %copy-start.2 = (f32[16,8,1024]{2,1,0:T(8,128)S(1)}, f32[16,8,1024]{2,1,0:T(8,128)}, u32[]{:S(2)}) copy-start(f32[16,8,1024]{2,1,0:T(8,128)} %param.6) | copy-start | bytes 1572868
  3.8 1.0 %copy-start.3 = (f32[16,8,1024]{2,1,0:T(8,128)S(1)}, f32[16,8,1024]{2,1,0:T(8,128)}, u32[]{:S(2)}) copy-start(f32[16,8,1024]{2,1,0:T(8,128)} %param.7) | copy-start | bytes 1572868

commit v2 on v1

--- a/solution.py
+++ b/solution.py
@@ -92,7 +92,8 @@
 
 
 def kernel(
-    n_gy, n_gz, f_ref, vx_ref, vy_ref, vz_ref, out_ref, dt_ref,
+    n_gy, n_gz, f_hbm, vx_hbm, vy_hbm, vz_hbm, out_ref, dt_ref,
+    f_ref, vx_ref, vy_ref, vz_ref, load_sem,
     g0, g1, g2, sx, dx, off, ta, tb, sd, vx, vy, vz, fy, fz,
     fy_in, fz_in, part_y, part_z,
     halo_send, halo_recv, vel_send, vel_recv, flux_send, flux_recv,
@@ -101,6 +102,12 @@
     Z = f_ref.shape[0]
     T = sx.shape[2]
     Y = f_ref.shape[1] // T
+    loads = []
+    for i, (source, target) in enumerate(
+        ((f_hbm, f_ref), (vx_hbm, vx_ref), (vy_hbm, vy_ref), (vz_hbm, vz_ref))
+    ):
+        loads.append(pltpu.make_async_copy(source, target, load_sem.at[i]))
+        loads[-1].start()
     my = lax.axis_index("gy")
     mz = lax.axis_index("gz")
 
@@ -154,11 +161,8 @@
             total = total + 4.0 * f * (1.0 - f)
         return total
 
+    loads[0].wait()
     total = lax.fori_loop(0, Z, fill, jnp.zeros((T, LANES), jnp.float32))
-    pl.semaphore_wait(barrier, len(greeted))
-    halos0 = halo_copies(g0, 0)
-    for copy in halos0:
-        copy.start()
 
     def fill_velocity(z, peak):
         for y in range(Y):
@@ -171,9 +175,26 @@
             peak = jnp.maximum(peak, jnp.maximum(jnp.abs(a), jnp.maximum(jnp.abs(b), jnp.abs(c))))
         return peak
 
+    for copy in loads[1:]:
+        copy.wait()
     peak = lax.fori_loop(0, Z, fill_velocity, jnp.zeros((T, LANES), jnp.float32))
-    part_y[my, 0] = total
-    part_y[my, 1] = peak
+    first_row = lax.broadcasted_iota(jnp.int32, (T, LANES), 0) == 0
+
+    def joined(sums, peaks):
+        sums = jnp.broadcast_to(jnp.sum(sums, axis=0, keepdims=True), (T, LANES))
+        peaks = jnp.broadcast_to(jnp.max(peaks, axis=0, keepdims=True), (T, LANES))
+        return jnp.where(first_row, sums, peaks)
+
+    def gathered(part, count):
+        sums = part[0]
+        peaks = part[0]
+        for i in range(1, count):
+            sums = sums + part[i]
+            peaks = jnp.maximum(peaks, part[i])
+        return jnp.where(first_row, sums, 0.0), jnp.where(first_row, 0.0, peaks)
+
+    part_y[my] = joined(total, peak)
+    pl.semaphore_wait(barrier, len(greeted))
     vel_copies = [
         pltpu.make_async_remote_copy(
             src_ref=vy.at[:, pl.ds(Y, 1)], dst_ref=vy.at[:, pl.ds(0, 1)],
@@ -199,6 +220,9 @@
 
     y_parts = part_copies(part_y, my, py_send, py_recv, n_gy, True)
     for copy in y_parts:
+        copy.start()
+    halos0 = halo_copies(g0, 0)
+    for copy in halos0:
         copy.start()
     for copy in vel_copies:
         copy.start()
@@ -249,66 +273,53 @@
     half = (Y - 2) // 2
     quarter = Y // 2
 
-    def planes_inside(g, dim, low, high):
-        def body(z):
-            plane(g, dim, z, 1, 1, half)
-            plane(g, dim, z, 1 + half, 1, Y - 2 - half)
-        loop(low, high, body)
-
-    def planes_edge(g, dim):
-        for_rows_edge(lambda z, y, kz, ky: plane(g, dim, z, y, kz, ky))
-
-    def for_rows_edge(body):
-        def ends(i):
+    def ends(body, low, high):
+        count = high - low
+
+        def step(i):
             z = i * (Z - 1)
-            body(z, 0, 1, quarter)
-            body(z, quarter, 1, Y - quarter)
-        loop(0, 2, ends)
-
-        def sides(i):
-            z = 1 + 2 * i
+            body(z, low, 1, count // 2)
+            body(z, low + count // 2, 1, count - count // 2)
+        loop(0, 2, step)
+
+    def sides(body, low, high):
+        def step(i):
+            z = low + 2 * i
             body(z, 0, 2, 1)
             body(z, Y - 1, 2, 1)
-        loop(0, (Z - 2) // 2, sides)
-
-    def for_rows_inside(body):
+        loop(0, (high - low) // 2, step)
+
+    def inside(body, low, high, first=1, last=None):
+        count = (Y - 1 if last is None else last) - first
+
         def step(z):
-            body(z, 1, 1, half)
-            body(z, 1 + half, 1, Y - 2 - half)
-        loop(1, Z - 1, step)
-
-    def for_rows(body):
-        def step(z):
-            body(z, 0, 1, quarter)
-            body(z, quarter, 1, Y - quarter)
-        loop(0, Z, step)
+            if count > 4:
+                body(z, first, 1, count // 2)
+                body(z, first + count // 2, 1, count - count // 2)
+            else:
+                body(z, first, 1, count)
+        loop(low, high, step)
+
+    def planes(g, dim):
+        return lambda z, y, kz, ky: plane(g, dim, z, y, kz, ky)
 
     smooth_inside(g0)
-    planes_inside(g0, 2, 1, Z // 2)
+    inside(planes(g0, 2), 1, Z // 2)
     for copy in y_parts:
         copy.wait()
-    sums = part_y[0, 0]
-    peaks = part_y[0, 1]
-    for i in range(1, n_gy):
-        sums = sums + part_y[i, 0]
-        peaks = jnp.maximum(peaks, part_y[i, 1])
-    part_z[mz, 0] = sums
-    part_z[mz, 1] = peaks
+    part_z[mz] = joined(*gathered(part_y, n_gy))
     z_parts = part_copies(part_z, mz, pz_send, pz_recv, n_gz, False)
     for copy in z_parts:
         copy.start()
-    planes_inside(g0, 2, Z // 2, Z - 1)
+    inside(planes(g0, 2), Z // 2, Z - 1)
     for copy in halos0:
         copy.wait()
     smooth_ghosts(g0)
-    planes_edge(g0, 2)
+    sides(planes(g0, 2), 0, Z)
+    ends(planes(g0, 2), 1, Y - 1)
     for copy in z_parts:
         copy.wait()
-    sums = part_z[0, 0]
-    peaks = part_z[0, 1]
-    for i in range(1, n_gz):
-        sums = sums + part_z[i, 0]
-        peaks = jnp.maximum(peaks, part_z[i, 1])
+    sums, peaks = gathered(part_z, n_gz)
     cells_all = float(Z * Y * T * LANES * n_gy * n_gz)
     share = jnp.broadcast_to(jnp.sum(sums, keepdims=True), (T, LANES)) / cells_all
     umax = jnp.broadcast_to(jnp.max(peaks, keepdims=True), (T, LANES))
@@ -331,20 +342,21 @@
             1.0 - cross + x_prev(cross)
         )
 
-    for_rows_edge(x_update)
+    sides(x_update, 0, Z)
+    ends(x_update, 1, Y - 1)
     halos1 = halo_copies(g1, 1)
     for copy in halos1:
         copy.start()
-    for_rows_inside(x_update)
+    inside(x_update, 1, Z - 1)
     for copy in vel_copies:
         copy.wait()
 
     smooth_inside(g1)
-    planes_inside(g1, 1, 1, Z - 1)
+    inside(planes(g1, 1), 1, Z - 1)
     for copy in halos1:
         copy.wait()
     smooth_ghosts(g1)
-    planes_edge(g1, 1)
+    sides(planes(g1, 1), 0, Z)
 
     def own_flux(velocity, where, at_face, least):
         cross = dt * velocity[at_face]
@@ -375,6 +387,7 @@
     )
     for copy in y_flux:
         copy.start()
+    ends(planes(g1, 1), 1, Y - 1)
 
     def between(velocity, at_face, below, above):
         cross = dt * velocity[at_face]
@@ -392,6 +405,18 @@
                 vy, (rows, pl.ds(low, count)), (rows, pl.ds(low - 1, count)), (rows, pl.ds(low, count))
             )
     loop(0, Z, y_inside)
+
+    def y_update(z, y, kz, ky):
+        rows = pl.ds(z, kz)
+        low, high = pl.ds(y, ky), pl.ds(y + 1, ky)
+        at_cells = (pl.ds(z + 1, kz), pl.ds(y + 1, ky))
+        g2[at_cells] = (g1[at_cells] - fy[rows, high] + fy[rows, low]) / (
+            1.0 - dt * vy[rows, high] + dt * vy[rows, low]
+        )
+
+    inside(y_update, 0, Z)
+    loop(1, Z + 1, lambda z: smooth_rows(g2, z, 2, 1, Y - 2))
+    inside(planes(g2, 0), 1, Z - 1, 2, Y - 2)
     for copy in y_flux:
         copy.wait()
 
@@ -400,27 +425,25 @@
         fy[rows, pl.ds(0, 1)] = fy[rows, pl.ds(0, 1)] + fy_in[0, rows]
         fy[rows, pl.ds(Y, 1)] = fy[rows, pl.ds(Y, 1)] + fy_in[1, rows]
     loop(0, Z // 4, y_merge)
-
-    def y_update(z, y, kz, ky):
-        rows = pl.ds(z, kz)
-        low, high = pl.ds(y, ky), pl.ds(y + 1, ky)
-        inside = (pl.ds(z + 1, kz), pl.ds(y + 1, ky))
-        g2[inside] = (g1[inside] - fy[rows, high] + fy[rows, low]) / (
-            1.0 - dt * vy[rows, high] + dt * vy[rows, low]
-        )
-
-    for_rows_edge(y_update)
+    sides(y_update, 0, Z)
     halos2 = halo_copies(g2, 2)
     for copy in halos2:
         copy.start()
-    for_rows_inside(y_update)
-
-    smooth_inside(g2)
-    planes_inside(g2, 0, 1, Z - 1)
+
+    def smooth_sides(z):
+        smooth_rows(g2, z, 1, 1, 1)
+        smooth_rows(g2, z, Y, 1, 1)
+    loop(1, Z + 1, smooth_sides)
+
+    def near_sides(i):
+        z = 1 + 2 * i
+        plane(g2, 0, z, 1, 2, 1)
+        plane(g2, 0, z, Y - 2, 2, 1)
+    loop(0, (Z - 2) // 2, near_sides)
     for copy in halos2:
         copy.wait()
     smooth_ghosts(g2)
-    planes_edge(g2, 0)
+    ends(planes(g2, 0), 0, Y)
 
     def z_ends(i):
         cols = pl.ds(2 * i, 2)
@@ -431,6 +454,7 @@
     z_flux = flux_copies(fz, fz_in, 1, [(pl.ds(Z, 1),), (pl.ds(0, 1),)], [(1, 0), (-1, 0)])
     for copy in z_flux:
         copy.start()
+    sides(planes(g2, 0), 1, Z - 1)
 
     def z_inside(z):
         face, below = pl.ds(z, 1), pl.ds(z - 1, 1)
@@ -474,21 +498,22 @@
                 jax.ShapeDtypeStruct((Z, T * Y, LANES), jnp.float32),
                 jax.ShapeDtypeStruct((1, 1), jnp.float32),
             ),
-            in_specs=[pl.BlockSpec(memory_space=pltpu.VMEM)] * 4,
+            in_specs=[pl.BlockSpec(memory_space=pltpu.HBM)] * 4,
             out_specs=(
                 pl.BlockSpec(memory_space=pltpu.VMEM),
                 pl.BlockSpec(memory_space=pltpu.SMEM),
             ),
             scratch_shapes=[
+                *[pltpu.VMEM((Z, T * Y, LANES), jnp.float32)] * 4, dma((4,)),
                 padded, padded, padded, padded, padded,
                 plain, plain, plain, plain,
                 plain, rows(Z, Y + 1), rows(Z + 1, Y), rows(Z, Y + 1), rows(Z + 1, Y),
-                rows(2, Z, 1), rows(2, 1, Y), rows(n_gy, 2), rows(n_gz, 2),
+                rows(2, Z, 1), rows(2, 1, Y), rows(n_gy), rows(n_gz),
                 dma((3, 8)), dma((3, 8)), dma((2,)), dma((2,)), dma((2, 2)), dma((2, 2)),
                 dma((n_gy - 1,)), dma((n_gy - 1,)), dma((n_gz - 1,)), dma((n_gz - 1,)),
             ],
             compiler_params=pltpu.CompilerParams(
-                collective_id=0, has_side_effects=True, vmem_limit_bytes=32 * 1024 * 1024
+                collective_id=0, has_side_effects=True, vmem_limit_bytes=67043328
             ),
         )(*[split(block) for block in blocks])
         field = field.reshape(Z, T, Y, LANES).transpose(0, 2, 1, 3).reshape(Z, Y, X)

time: 52.9 us -> 48.1 us (0.909)
  local copies, waits for them, and re-layouts: 4.95 us -> 1.89 us
  Pallas kernels: 45.2 us -> 43.6 us
    unnamed x9 -> x1, local copies, waits for them, and re-layouts: 4.95 us -> 1.89 us
    pallas_call x1, Pallas kernels: 45.2 us -> 43.6 us  [shards(): pl.pallas_call(functools.partial(kernel, n_gy, n_gz), out_shape=(jax.Shap...]
where the time goes in v2:
time: 48.1 us; the launch traced here: 47.9 us
  Pallas kernels  43.6 us (91%)
  between operations  2.34 us (5%)
  local copies, waits for them, and re-layouts  1.89 us (4%)
    pallas_call x1, Pallas kernels, shards(): pl.pallas_call(functools.partial(kernel, n_gy, n_gz), out_shape=(jax.Shap...  43.6 us
    unnamed x1, local copies, waits for them, and re-layouts  1.89 us

profile of v2, /device:TPU:0, one launch (start us, length us, event | category | flops | bytes accessed | tf_op | source)
XLA Modules:
  0.0 47.9 jit_solution(4037635285112893677)
XLA Ops:
  0.6 43.6 %shard_map.59 = (f32[16,64,128]{2,1,0:T(8,128)}, f32[1,1]{1,0:T(1,128)}) custom-call(f32[16,64,128]{2,1,0:T(8,128)} %bitcast.27, f32[16,64,128]{2,1,0:T(8,128)} %bitcast.28, f32[16,64,128]{2,1,0:T(8,128)} %bitcast.29, f32[16,64,128]{2,1,0:T(8,128)} %bitcast.30), custom_call_target="tpu_custom_call" | custom-call | tf_op jit(solution)/shard_map/pallas_call | solution.py:495
  44.3 1.9 %copy.8 = f32[16,8,1024]{2,1,0:T(8,128)} copy(f32[16,8,1024]{2,1,0:T(8,128)} %bitcast.26) | data formatting | bytes 1048576

commit v3 on v2

--- a/solution.py
+++ b/solution.py
@@ -9,6 +9,7 @@
 
 NEWTON = 5
 LANES = 128
+GROUP = 8
 
 tilt_floor = 0.1
 courant = 0.45
@@ -126,11 +127,21 @@
     def rows_of(ref, z, y):
         return ref[z, pl.ds(y, T, stride=Y), :]
 
+    def gather(low, high, body, carry):
+        count = high - low
+        grouped = max(u for u in range(1, GROUP + 1) if count % u == 0)
+
+        def step(i, carry):
+            for u in range(grouped):
+                carry = body(low + i * grouped + u, carry)
+            return carry
+        return lax.fori_loop(0, count // grouped, step, carry)
+
     def loop(low, high, body):
         def step(i, carry):
             body(i)
             return carry
-        lax.fori_loop(low, high, step, 0)
+        gather(low, high, step, 0)
 
     def span(side, count):
         if side == 0:
@@ -162,7 +173,7 @@
         return total
 
     loads[0].wait()
-    total = lax.fori_loop(0, Z, fill, jnp.zeros((T, LANES), jnp.float32))
+    total = gather(0, Z, fill, jnp.zeros((T, LANES), jnp.float32))
 
     def fill_velocity(z, peak):
         for y in range(Y):
@@ -177,7 +188,7 @@
 
     for copy in loads[1:]:
         copy.wait()
-    peak = lax.fori_loop(0, Z, fill_velocity, jnp.zeros((T, LANES), jnp.float32))
+    peak = gather(0, Z, fill_velocity, jnp.zeros((T, LANES), jnp.float32))
     first_row = lax.broadcasted_iota(jnp.int32, (T, LANES), 0) == 0
 
     def joined(sums, peaks):

time: 48.1 us -> 40.3 us (0.84)
  Pallas kernels: 43.6 us -> 35.9 us
    pallas_call x1, Pallas kernels: 43.6 us -> 35.9 us  [shards(): pl.pallas_call(functools.partial(kernel, n_gy, n_gz), out_shape=(jax.Shap...]
where the time goes in v3:
time: 40.3 us; the launch traced here: 40.1 us
  Pallas kernels  35.9 us (89%)
  between operations  2.34 us (6%)
  local copies, waits for them, and re-layouts  1.89 us (5%)
    pallas_call x1, Pallas kernels, shards(): pl.pallas_call(functools.partial(kernel, n_gy, n_gz), out_shape=(jax.Shap...  35.9 us
    unnamed x1, local copies, waits for them, and re-layouts  1.89 us

profile of v3, /device:TPU:0, one launch (start us, length us, event | category | flops | bytes accessed | tf_op | source)
XLA Modules:
  0.0 40.1 jit_solution(17696799916042711384)
XLA Ops:
  0.6 35.9 %shard_map.59 = (f32[16,64,128]{2,1,0:T(8,128)}, f32[1,1]{1,0:T(1,128)}) custom-call(f32[16,64,128]{2,1,0:T(8,128)} %bitcast.27, f32[16,64,128]{2,1,0:T(8,128)} %bitcast.28, f32[16,64,128]{2,1,0:T(8,128)} %bitcast.29, f32[16,64,128]{2,1,0:T(8,128)} %bitcast.30), custom_call_target="tpu_custom_call" | custom-call | tf_op jit(solution)/shard_map/pallas_call | solution.py:506
  36.6 1.9 %copy.8 = f32[16,8,1024]{2,1,0:T(8,128)} copy(f32[16,8,1024]{2,1,0:T(8,128)} %bitcast.26) | data formatting | bytes 1048576

commit v4 on v3

--- a/solution.py
+++ b/solution.py
@@ -9,7 +9,7 @@
 
 NEWTON = 5
 LANES = 128
-GROUP = 8
+GROUP = 16
 
 tilt_floor = 0.1
 courant = 0.45

time: 40.3 us -> 40.4 us (level)
  no operation moved by 1% of the time
where the time goes in v4:
time: 40.4 us; the launch traced here: 40.1 us
  Pallas kernels  35.9 us (89%)
  between operations  2.34 us (6%)
  local copies, waits for them, and re-layouts  1.89 us (5%)
    pallas_call x1, Pallas kernels, shards(): pl.pallas_call(functools.partial(kernel, n_gy, n_gz), out_shape=(jax.Shap...  35.9 us
    unnamed x1, local copies, waits for them, and re-layouts  1.89 us

profile of v4, /device:TPU:0, one launch (start us, length us, event | category | flops | bytes accessed | tf_op | source)
XLA Modules:
  0.0 40.1 jit_solution(11132029997828753021)
XLA Ops:
  0.6 35.9 %shard_map.59 = (f32[16,64,128]{2,1,0:T(8,128)}, f32[1,1]{1,0:T(1,128)}) custom-call(f32[16,64,128]{2,1,0:T(8,128)} %bitcast.27, f32[16,64,128]{2,1,0:T(8,128)} %bitcast.28, f32[16,64,128]{2,1,0:T(8,128)} %bitcast.29, f32[16,64,128]{2,1,0:T(8,128)} %bitcast.30), custom_call_target="tpu_custom_call" | custom-call | tf_op jit(solution)/shard_map/pallas_call | solution.py:506
  36.6 1.9 %copy.8 = f32[16,8,1024]{2,1,0:T(8,128)} copy(f32[16,8,1024]{2,1,0:T(8,128)} %bitcast.26) | data formatting | bytes 1048576
